TPU v7x, 32 devices: a 4x2x2 block of a 4x4x8 slice. The times are simulated.
32 devices in a mesh: dp: 4 (over y, z), sp: 8 (over x, core).
Axes of the slice: x: 4, y: 2, z: 2, core: 2. Of those that a mesh axis runs over, the one named last changes fastest.
The devices are a block of a 4x4x8 slice.
Arguments:
- x_patch: bfloat16 [64, 4096, 1024], P('dp', 'sp'), parts along dimension 0
- w_tok1: bfloat16 [4096, 512], P('sp')
- b_tok1: float32 [512], P('sp')
- w_tok2: bfloat16 [512, 4096], P(None, 'sp')
- b_tok2: float32 [4096], P('sp')
- w_ch1: bfloat16 [1024, 4096], replicated
- b_ch1: float32 [4096], replicated
- w_ch2: bfloat16 [4096, 1024], replicated
- b_ch2: float32 [1024], replicated
- ln1_gain: float32 [1024], replicated
- ln1_bias: float32 [1024], replicated
- ln2_gain: float32 [1024], replicated
- ln2_bias: float32 [1024], replicated
Outputs:
- output: bfloat16 [64, 4096, 1024], P('dp', 'sp'), parts along dimension 0
There are 4 independent parts. A program takes and returns all parts, laid end to end along the dimension named above; an argument that names none is the same for every part.
All inputs are finite; a program needn't handle non-finite values.
Results may differ from a plain program's by a relative error of at most 0.00987663.
Values are sent between devices in bfloat16 or wider.
A program may use at most 768 MiB of HBM per device.

v0:
```python
import jax
import jax.numpy as jnp
from jax import lax
from jax.sharding import PartitionSpec as P

LN_EPS = 1e-6


def layer_norm(values, ln_gain, ln_bias):
    mean_val = jnp.mean(values, axis=-1, keepdims=True)
    centred = values - mean_val
    var_val = jnp.mean(centred * centred, axis=-1, keepdims=True)
    return centred * lax.rsqrt(var_val + LN_EPS) * ln_gain + ln_bias


def channel_mix(x_mid, w_ch1, b_ch1, w_ch2, b_ch2, ln2_gain, ln2_bias):
    mid_wide = x_mid.astype(jnp.float32)
    normed_two = layer_norm(mid_wide, ln2_gain, ln2_bias).astype(jnp.bfloat16)
    ch_pre = jnp.einsum("bsc,cf->bsf", normed_two, w_ch1, preferred_element_type=jnp.float32) + b_ch1
    ch_act = jax.nn.gelu(ch_pre).astype(jnp.bfloat16)
    ch_out = jnp.einsum("bsf,fc->bsc", ch_act, w_ch2, preferred_element_type=jnp.float32) + b_ch2
    return (mid_wide + ch_out).astype(jnp.bfloat16)


def solution(mesh):
    row_spec = P("dp", "sp", None)

    def local_layer(x_blk, w1_rows, b1_part, w2_cols, b2_part, w_ch1, b_ch1, w_ch2, b_ch2, ln1_gain, ln1_bias, ln2_gain, ln2_bias):
        x_wide = x_blk.astype(jnp.float32)
        normed = layer_norm(x_wide, ln1_gain, ln1_bias).astype(jnp.bfloat16)
        part_pre = jnp.einsum("bsc,sd->bdc", normed, w1_rows, preferred_element_type=jnp.float32)
        tok_pre = lax.psum_scatter(part_pre, "sp", scatter_dimension=1, tiled=True) + b1_part[None, :, None]
        tok_act = jax.nn.gelu(tok_pre).astype(jnp.bfloat16)
        act_full = lax.all_gather(tok_act, "sp", axis=1, tiled=True)
        tok_out = jnp.einsum("bdc,ds->bsc", act_full, w2_cols, preferred_element_type=jnp.float32) + b2_part[None, :, None]
        x_mid = (x_wide + tok_out).astype(jnp.bfloat16)
        return channel_mix(x_mid, w_ch1, b_ch1, w_ch2, b_ch2, ln2_gain, ln2_bias)

    in_specs = (row_spec, P("sp", None), P("sp"), P(None, "sp"), P("sp"), P(None, None), P(None), P(None, None), P(None), P(None), P(None), P(None), P(None))
    return jax.shard_map(local_layer, mesh=mesh, in_specs=in_specs, out_specs=row_spec, check_vma=False)
```

profile of v0, /device:TPU:81, one launch (start us, length us, event | category | flops | bytes accessed | tf_op | source)
XLA Modules:
  0.0 587.7 jit_solution(17255997997323537284)
XLA Ops:
  6.5 0.0 copy-start
  6.6 0.0 copy-start.6
  6.6 0.0 copy-start.7
  6.6 0.0 copy-start.4
  6.6 0.1 reduce-scatter.2.cloned.1.call-start
  6.6 21.7 %copy.19 = bf16[16,512,1024]{1,2,0:T(8,128)(2,1)} copy(bf16[16,512,1024]{2,1,0:T(8,128)(2,1)} %param.13) | data formatting | bytes 33554432 | tf_op args[0]
  28.4 6.7 %convert_reduce_fusion.1 = f32[16,512]{1,0:T(8,128)S(1)} fusion(bf16[16,512,1024]{1,2,0:T(8,128)(2,1)} %copy.19), kind=kLoop, calls=%fused_computation.15 | loop fusion | flops 16769024 | bytes 16809984 | tf_op jit(solution)/shard_map/reduce_sum | solution.py:10
  35.1 7.4 %fusion.18 = f32[16,512]{1,0:T(8,128)S(1)} fusion(bf16[16,512,1024]{1,2,0:T(8,128)(2,1)} %copy.19, f32[16,512]{1,0:T(8,128)S(1)} %broadcast_multiply_fusion.1), kind=kLoop, calls=%fused_computation.24 | loop fusion | flops 33546240 | bytes 16842752 | tf_op jit(solution)/shard_map/reduce_sum | solution.py:12
  42.6 0.0 copy-done.6
  42.6 0.0 copy-done.7
  42.6 0.0 copy-done.4
  42.6 18.9 %fusion.40 = f32[16,512,1024]{1,2,0:T(8,128)} fusion(bf16[16,512,1024]{1,2,0:T(8,128)(2,1)} %copy.19, f32[1024]{0:T(1024)S(1)} %copy-done.6, f32[1024]{0:T(1024)S(1)} %copy-done.7, f32[16,512]{1,0:T(8,128)S(1)} %add_rsqrt_fusion.1, f32[16,512]{1,0:T(8,128)S(1)} %broadcast_multiply_fusion.1, bf16[512,512]{1,0:T(8,128)(2,1)S(1)} %copy-done.4), kind=kOutput, calls=%fused_computation.42 | convolution fusion | flops 8640266240 | bytes 50929664 | tf_op jit(solution)/shard_map/bsc,sd->bdc/dot_general | solution.py:31
  61.5 33.1 %copy.20 = f32[16,512,1024]{2,0,1:T(8,128)} copy(f32[16,512,1024]{1,2,0:T(8,128)} %fusion.40) | data formatting | bytes 67108864 | tf_op jit(solution)/shard_map/bsc,sd->bdc/transpose | solution.py:31
  94.6 0.0 copy-start.3
  94.6 0.0 copy-start.11
  94.6 0.1 reduce-scatter.2.cloned.1.call-update
  94.7 0.2 all-gather.2.cloned.1.call-start
  94.9 171.0 %reduce-scatter.2.cloned.1.call-done = f32[16,64,1024]{2,0,1:T(8,128)} async-done(((f32[16,512,1024]{2,0,1:T(8,128)}), f32[16,64,1024]{2,0,1:T(8,128)}) %reduce-scatter.2.cloned.1.call-update) | async-done | bytes 4194320 | tf_op jit(solution)/shard_map/reduce_scatter | solution.py:32
  265.9 0.0 copy-done.3
  265.9 5.1 fusion.54
  271.0 0.1 all-gather.2.cloned.1.call-update
  271.0 0.0 copy-start.8
  271.0 0.0 copy-start.9
  271.0 82.7 %all-gather.2.cloned.1.call-done = bf16[16,512,1024]{2,0,1:T(8,128)(2,1)} async-done(((bf16[16,64,1024]{2,0,1:T(8,128)(2,1)}), bf16[16,512,1024]{2,0,1:T(8,128)(2,1)}) %all-gather.2.cloned.1.call-update) | async-done | bytes 16777232 | tf_op jit(solution)/shard_map/all_gather | solution.py:34
  353.8 0.0 copy-done
  353.8 0.0 copy-done.11
  353.8 25.4 %convert_reduce_fusion = (f32[16,512]{1,0:T(8,128)S(1)}, bf16[16,512,1024]{1,2,0:T(8,128)(2,1)S(1)}) fusion(f32[512]{0:T(512)S(1)} %copy-done.11, bf16[512,512]{1,0:T(8,128)(2,1)S(1)} %copy-done, bf16[16,512,1024]{2,0,1:T(8,128)(2,1)} %all-gather.2.cloned.1.call-done, bf16[16,512,1024]{1,2,0:T(8,128)(2,1)} %copy.19), kind=kOutput, calls=%fused_computation.12 | convolution fusion | flops 8640258048 | bytes 50890752 | tf_op jit(solution)/shard_map/bdc,ds->bsc/dot_general | solution.py:35
  379.1 0.0 copy-start.2
  379.2 6.1 %copy-done.2 = bf16[16,512,1024]{1,2,0:T(8,128)(2,1)} copy-done((bf16[16,512,1024]{1,2,0:T(8,128)(2,1)}, bf16[16,512,1024]{1,2,0:T(8,128)(2,1)S(1)}, u32[]{:S(2)}) %copy-start.2) | copy-done | bytes 16777240
  385.3 4.6 fusion.14
  389.9 0.0 copy-done.8
  389.9 0.0 copy-done.9
  389.9 0.0 copy-start.5
  389.9 0.0 copy-start.10
  389.9 83.3 %fusion.26 = f32[16,512,4096]{2,1,0:T(8,128)} fusion(bf16[16,512,1024]{1,2,0:T(8,128)(2,1)} %copy-done.2, f32[1024]{0:T(1024)S(1)} %copy-done.8, f32[1024]{0:T(1024)S(1)} %copy-done.9, f32[16,512]{1,0:T(8,128)S(1)} %add_rsqrt_fusion, f32[16,512]{1,0:T(8,128)S(1)} %broadcast_multiply_fusion, bf16[1024,4096]{1,0:T(8,128)(2,1)} %param.18), kind=kOutput, calls=%fused_computation.31 | convolution fusion | flops 68769808384 | bytes 159457280 | tf_op jit(solution)/shard_map/bsc,cf->bsf/dot_general | solution.py:19
  473.3 0.0 copy-done.5
  473.3 0.0 copy-done.10
  473.3 0.0 copy-start.1
  473.3 86.0 %fusion.23 = bf16[16,512,1024]{1,2,0:T(8,128)(2,1)} fusion(bf16[16,512,1024]{1,2,0:T(8,128)(2,1)} %copy-done.2, f32[1024]{0:T(1024)S(1)} %copy-done.10, f32[16,512,4096]{2,1,0:T(8,128)} %fusion.26, f32[4096]{0:T(1024)S(1)} %copy-done.5, bf16[4096,1024]{1,0:T(8,128)(2,1)} %param.20), kind=kOutput, calls=%fused_computation.29 | convolution fusion | flops 69088575488 | bytes 176181248 | tf_op jit(solution)/shard_map/bsf,fc->bsc/dot_general | solution.py:21
  559.2 21.5 %copy.24 = bf16[16,512,1024]{2,1,0:T(8,128)(2,1)} copy(bf16[16,512,1024]{1,2,0:T(8,128)(2,1)} %fusion.23) | data formatting | bytes 33554432 | tf_op jit(solution)/shard_map/convert_element_type | solution.py:22
  580.8 0.0 copy-done.1
  (4 shorter events, 0.0 us)
Async XLA Ops:
  6.5 347.2 %copy-start = (bf16[512,512]{1,0:T(8,128)(2,1)S(1)}, bf16[512,512]{1,0:T(8,128)(2,1)}, u32[]{:S(2)}) copy-start(bf16[512,512]{1,0:T(8,128)(2,1)} %param.16) | copy-start | bytes 1572868
  6.6 36.0 %copy-start.6 = (f32[1024]{0:T(1024)S(1)}, f32[1024]{0:T(1024)}, u32[]{:S(2)}) copy-start(f32[1024]{0:T(1024)} %param.23) | copy-start | bytes 12292
  6.6 36.0 %copy-start.7 = (f32[1024]{0:T(1024)S(1)}, f32[1024]{0:T(1024)}, u32[]{:S(2)}) copy-start(f32[1024]{0:T(1024)} %param.22) | copy-start | bytes 12292
  6.6 36.0 %copy-start.4 = (bf16[512,512]{1,0:T(8,128)(2,1)S(1)}, bf16[512,512]{1,0:T(8,128)(2,1)}, u32[]{:S(2)}) copy-start(bf16[512,512]{1,0:T(8,128)(2,1)} %param.14) | copy-start | bytes 1572868
  6.6 259.3 %reduce-scatter.2.cloned.1.call-start = ((), (), s32[]{:S(2)}) async-start(), calls=%async_computation.1 | async-start | bytes 37748736 | tf_op jit(solution)/shard_map/reduce_scatter | solution.py:32
  94.6 171.3 %copy-start.3 = (f32[64]{0:T(128)S(1)}, f32[64]{0:T(128)}, u32[]{:S(2)}) copy-start(f32[64]{0:T(128)} %param.15) | copy-start | bytes 772
  94.6 259.2 %copy-start.11 = (f32[512]{0:T(512)S(1)}, f32[512]{0:T(512)}, u32[]{:S(2)}) copy-start(f32[512]{0:T(512)} %param.17) | copy-start | bytes 6148
  94.7 259.1 %all-gather.2.cloned.1.call-start = ((), (), s32[]{:S(2)}) async-start(), calls=%async_computation.2 | async-start | bytes 18874368 | tf_op jit(solution)/shard_map/all_gather | solution.py:34
  271.0 118.9 %copy-start.8 = (f32[1024]{0:T(1024)S(1)}, f32[1024]{0:T(1024)}, u32[]{:S(2)}) copy-start(f32[1024]{0:T(1024)} %param.25) | copy-start | bytes 12292
  271.0 118.9 %copy-start.9 = (f32[1024]{0:T(1024)S(1)}, f32[1024]{0:T(1024)}, u32[]{:S(2)}) copy-start(f32[1024]{0:T(1024)} %param.24) | copy-start | bytes 12292
  379.1 6.2 %copy-start.2 = (bf16[16,512,1024]{1,2,0:T(8,128)(2,1)}, bf16[16,512,1024]{1,2,0:T(8,128)(2,1)S(1)}, u32[]{:S(2)}) copy-start(bf16[16,512,1024]{1,2,0:T(8,128)(2,1)S(1)} %get-tuple-element.6) | copy-start | bytes 50331652
  389.9 83.4 %copy-start.5 = (f32[4096]{0:T(1024)S(1)}, f32[4096]{0:T(1024)}, u32[]{:S(2)}) copy-start(f32[4096]{0:T(1024)} %param.19) | copy-start | bytes 49156
  389.9 83.3 %copy-start.10 = (f32[1024]{0:T(1024)S(1)}, f32[1024]{0:T(1024)}, u32[]{:S(2)}) copy-start(f32[1024]{0:T(1024)} %param.21) | copy-start | bytes 12292
  473.3 107.5 %copy-start.1 = (bf16[512,512]{1,0:T(8,128)(2,1)S(1)}, bf16[512,512]{1,0:T(8,128)(2,1)}, u32[]{:S(2)}) copy-start(bf16[512,512]{1,0:T(8,128)(2,1)} %param.16) | copy-start | bytes 1572868
Sparse Core Ops, SparseCore 0:
  94.8 171.0 reduce-scatter.1
  271.1 82.5 all-gather.1
where the time goes:
time: 589 us; the launch traced here: 588 us
  waiting for transfers between devices  254 us (43%)
  matrix products  214 us (36%)
  local copies, waits for them, and re-layouts  82.6 us (14%)
  other arithmetic  23.8 us (4%)
  between operations  13.6 us (2%)
    reduce_scatter x1, waiting for transfers between devices, local_layer(): lax.psum_scatter(part_pre, 'sp', scatter_dimension=1, tiled=True)  171 us
    dot_general x1, matrix products, channel_mix(): jnp.einsum('bsf,fc->bsc', ch_act, w_ch2, preferred_element_type=jnp.float32)  86 us
    dot_general x1, matrix products, channel_mix(): jnp.einsum('bsc,cf->bsf', normed_two, w_ch1, preferred_element_type=jnp.f...  83.3 us
    all_gather x1, waiting for transfers between devices, local_layer(): act_full = lax.all_gather(tok_act, 'sp', axis=1, tiled=True)  82.7 us
    transpose x1, local copies, waits for them, and re-layouts, local_layer(): jnp.einsum('bsc,sd->bdc', normed, w1_rows, preferred_element_type=jnp.flo...  33.1 us
    unnamed x25, local copies, waits for them, and re-layouts  27.9 us
    dot_general x1, matrix products, local_layer(): jnp.einsum('bdc,ds->bsc', act_full, w2_cols, preferred_element_type=jnp.f...  25.4 us
    convert_element_type x1, local copies, waits for them, and re-layouts, channel_mix(): return (mid_wide + ch_out).astype(jnp.bfloat16)  21.5 us
  transfers between devices with their start and end apart: 2, of which 2 were waited for; matrix products, arithmetic and copies ran while one was open for 0% of the time, Pallas kernels for 0%

commit v1 on v0

v1 whole, which is shorter than its diff:
```python
import functools

import jax
import jax.numpy as jnp
from jax import lax
from jax.experimental import pallas as pl
from jax.experimental.pallas import tpu as pltpu
from jax.sharding import PartitionSpec as P

LN_EPS = 1e-6
MESH = pl.DeviceIdType.MESH
F32 = jnp.float32
BF16 = jnp.bfloat16
LAG = 6
XS = LAG + 3
GS = LAG
CW = 512
LB = 64
TANH_A = 0.7978845608028654
TANH_B = 0.7978845608028654 * 0.044715


def gelu(a):
    half = 0.5 * a
    return half + half * jnp.tanh(a * (TANH_A + TANH_B * (a * a)))


def norm(values, gain, bias):
    mean = jnp.mean(values, axis=-1, keepdims=True)
    centred = values - mean
    var = jnp.mean(centred * centred, axis=-1, keepdims=True)
    return centred * lax.rsqrt(var + LN_EPS) * gain + bias


def dot(a, b):
    return jnp.dot(a, b, preferred_element_type=F32)


def layer_kernel(n, x_hbm, w1_hbm, w2_hbm, wc1_hbm, wc2_hbm, b1_ref, b2_ref, bc1_ref, bc2_ref, g1_ref, o1_ref, g2_ref, o2_ref,
                 z_hbm, w1, w2, wc1, wc2, xs, us, part, sums, pair_in, hop1_out, hop1_in, hop2_out, hop2_in, gs,
                 x1s, vs, act0, act1, acc, zs,
                 w_sem, x_sem, z_sem, p_send, p_recv, h1_send, h1_recv, h2_send, h2_recv, a1_send, a1_recv, a2_send, a2_recv,
                 a3_send, a3_recv):
    images, rows, chans = x_hbm.shape
    own = b1_ref.shape[0]
    half_c = chans // 2
    wide = wc1.shape[1]
    chips = n // 2
    me = lax.axis_index("sp")
    core = lax.rem(me, 2)
    chip = me // 2
    chip_r = lax.rem(chip + 1, chips)
    chip_l = lax.rem(chip + chips - 1, chips)
    chip_o = lax.rem(chip + 2, chips)
    right = 2 * chip_r + core
    left = 2 * chip_l + core
    pair = 2 * chip + 1 - core
    opposite = 2 * chip_o + core

    def remote(src, dst, send, recv, to):
        return pltpu.make_async_remote_copy(src_ref=src, dst_ref=dst, send_sem=send, recv_sem=recv,
                                            device_id={"sp": to}, device_id_type=MESH)

    def x_copy(i):
        slot = lax.rem(i, XS)
        return pltpu.make_async_copy(x_hbm.at[i], xs.at[slot], x_sem.at[slot])

    def z_copy(i):
        slot = lax.rem(i, 2)
        return pltpu.make_async_copy(zs.at[slot], z_hbm.at[i], z_sem.at[slot])

    def w_copy(k, src, dst):
        return pltpu.make_async_copy(src, dst, w_sem.at[k])

    def chunk(q):
        return pl.ds(pl.multiple_of(q * own, own), own)

    def g_rows(slot, dev):
        return gs.at[slot, pl.ds(pl.multiple_of(dev * own, own), own), :]

    def pair_copy(i):
        slot = lax.rem(i, 2)
        return remote(part, pair_in.at[slot], p_send, p_recv.at[slot], pair)

    def hop1_copy(i, d):
        slot = lax.rem(i, 2)
        return remote(hop1_out.at[d], hop1_in.at[slot, d], h1_send.at[d], h1_recv.at[slot, d], (right, left)[d])

    def hop2_copy(i, d):
        slot = lax.rem(i, 2)
        return remote(hop2_out.at[d], hop2_in.at[slot, d], h2_send.at[d], h2_recv.at[slot, d], (right, left)[d])

    def gather1_copy(i, d):
        slot, par = lax.rem(i, GS), lax.rem(i, 2)
        mine = g_rows(slot, me)
        return remote(mine, mine, a1_send.at[d], a1_recv.at[par, d], (right, left, pair)[d])

    def gather2_copy(i, d):
        slot, par = lax.rem(i, GS), lax.rem(i, 2)
        source = (left, right, left, right)[d]
        if d < 2:
            block = gs.at[slot, pl.ds(pl.multiple_of(source * own, own), own), pl.ds(d * half_c, half_c)]
        else:
            block = g_rows(slot, source)
        return remote(block, block, a2_send.at[d], a2_recv.at[par, d], (right, left, pair, pair)[d])

    def gather3_copy(i):
        slot, par = lax.rem(i, GS), lax.rem(i, 2)
        block = g_rows(slot, opposite)
        return remote(block, block, a3_send, a3_recv.at[par], pair)

    def stage0(i):
        xslot, slot = lax.rem(i, XS), lax.rem(i, 3)
        for r in range(0, rows, LB):
            us[r:r + LB, :] = norm(xs[xslot, r:r + LB, :].astype(F32), g1_ref[...], o1_ref[...]).astype(BF16)
        side = part.shape[0]
        theirs = pl.ds(pl.multiple_of((1 - core) * side, side), side)
        mine = pl.ds(pl.multiple_of(core * side, side), side)
        for c in range(0, chans, 256):
            u = us[:, c:c + 256]
            part[:, c:c + 256] = dot(w1[theirs, :], u)
            sums[slot, :, c:c + 256] = dot(w1[mine, :], u)

    def stage1(i):
        slot, par = lax.rem(i, 3), lax.rem(i, 2)
        pair_copy(i).wait()
        for q in range(chips):
            r = slice(q * own, (q + 1) * own)
            sums[slot, r, :] = sums[slot, r, :] + pair_in[par, r, :]
        far = sums[slot, chunk(chip_o), :]
        hop1_out[0] = far[:, :half_c].astype(BF16)
        hop1_out[1] = far[:, half_c:].astype(BF16)

    def stage2(i):
        slot, par = lax.rem(i, 3), lax.rem(i, 2)
        for d in range(2):
            hop1_copy(i, d).wait()
        to_right = sums[slot, chunk(chip_r), :]
        hop2_out[0, :, :half_c] = (to_right[:, :half_c] + hop1_in[par, 0].astype(F32)).astype(BF16)
        hop2_out[0, :, half_c:] = to_right[:, half_c:].astype(BF16)
        to_left = sums[slot, chunk(chip_l), :]
        hop2_out[1, :, :half_c] = to_left[:, :half_c].astype(BF16)
        hop2_out[1, :, half_c:] = (to_left[:, half_c:] + hop1_in[par, 1].astype(F32)).astype(BF16)

    def stage3(i):
        slot, par = lax.rem(i, 3), lax.rem(i, 2)
        for d in range(2):
            hop2_copy(i, d).wait()
        h = sums[slot, chunk(chip), :] + hop2_in[par, 0].astype(F32) + hop2_in[par, 1].astype(F32) + b1_ref[...]
        gs[lax.rem(i, GS), chunk(me), :] = gelu(h).astype(BF16)

    def send1(i):
        for d in range(2):
            hop1_copy(i, d).start()

    def send2(i):
        for d in range(2):
            hop2_copy(i, d).start()

    def send3(i):
        for d in range(3):
            gather1_copy(i, d).start()

    def got(sem, region):
        pltpu.make_async_copy(region, region, sem).wait()

    def stage4(i):
        slot, par = lax.rem(i, GS), lax.rem(i, 2)
        for d in range(3):
            gather1_copy(i, d).wait_send()
            got(a1_recv.at[par, d], g_rows(slot, (left, right, pair)[d]))
        for d in range(4):
            gather2_copy(i, d).start()

    def stage5(i):
        slot, par = lax.rem(i, GS), lax.rem(i, 2)
        far = pl.ds(pl.multiple_of(opposite * own, own), own)
        for d in range(4):
            gather2_copy(i, d).wait_send()
        for d in range(2):
            got(a2_recv.at[par, d], gs.at[slot, far, pl.ds(d * half_c, half_c)])
        for d in range(2):
            got(a2_recv.at[par, 2 + d], g_rows(slot, 2 * (chip_l, chip_r)[d] + 1 - core))
        gather3_copy(i).start()

    def stage6_ready(i):
        slot, par = lax.rem(i, GS), lax.rem(i, 2)
        gather3_copy(i).wait_send()
        got(a3_recv.at[par], g_rows(slot, 2 * chip_o + 1 - core))

    def stage6(i):
        xslot, slot, zslot = lax.rem(i, XS), lax.rem(i, GS), lax.rem(i, 2)
        for r in range(0, rows, 256):
            for c in range(0, chans, 256):
                t = dot(w2[r:r + 256, :], gs[slot, :, c:c + 256]) + b2_ref[r:r + 256, :]
                x1s[r:r + 256, c:c + 256] = (xs[xslot, r:r + 256, c:c + 256].astype(F32) + t).astype(BF16)
            for q in range(r, r + 256, LB):
                vs[q:q + LB, :] = norm(x1s[q:q + LB, :].astype(F32), g2_ref[...], o2_ref[...]).astype(BF16)
        acts = (act0, act1)
        steps = wide // CW

        def up(k):
            for c in range(0, CW, 256):
                col = slice(k * CW + c, k * CW + c + 256)
                pre = dot(vs[...], wc1[:, col]) + bc1_ref[:, col]
                acts[k % 2][:, c:c + 256] = gelu(pre).astype(BF16)

        def down(k):
            for c in range(0, chans, 256):
                piece = dot(acts[k % 2][...], wc2[k * CW:(k + 1) * CW, c:c + 256])
                if k == 0:
                    acc[:, c:c + 256] = piece
                elif k < steps - 1:
                    acc[:, c:c + 256] = acc[:, c:c + 256] + piece
                else:
                    total = acc[:, c:c + 256] + piece + bc2_ref[:, c:c + 256]
                    zs[zslot, :, c:c + 256] = (x1s[:, c:c + 256].astype(F32) + total).astype(BF16)

        up(0)
        for k in range(1, steps):
            up(k)
            down(k - 1)
        down(steps - 1)

    def comm(t, guard):
        for k, stage in ((5, stage5), (4, stage4), (3, stage3), (2, stage2), (1, stage1)):
            guard(t - k, stage)
        for k, send in ((3, send3), (2, send2), (1, send1)):
            guard(t - k, send)

    def always(i, stage):
        stage(i)

    def guarded(i, stage):
        @pl.when(jnp.logical_and(i >= 0, i < images))
        def _():
            stage(i)

    x_copy(0).start()
    w_copy(0, w1_hbm, w1).start()
    barrier = pltpu.get_barrier_semaphore()
    for dev in (left, right, pair):
        pl.semaphore_signal(barrier, inc=1, device_id={"sp": dev}, device_id_type=MESH)
    pl.semaphore_wait(barrier, 3)
    x_copy(1).start()
    w_copy(0, w1_hbm, w1).wait()
    w_copy(1, w2_hbm, w2).start()
    w_copy(2, wc1_hbm, wc1).start()
    w_copy(3, wc2_hbm, wc2).start()

    @pl.loop(0, LAG)
    def _(t):
        comm(t, guarded)
        x_copy(t).wait()
        x_copy(t + 2).start()
        stage0(t)
        pair_copy(t).start()

    w_copy(1, w2_hbm, w2).wait()
    w_copy(2, wc1_hbm, wc1).wait()
    w_copy(3, wc2_hbm, wc2).wait()

    def z_free(i):
        @pl.when(i >= 2)
        def _():
            z_copy(i - 2).wait()

    @pl.loop(LAG, images)
    def _(t):
        stage6_ready(t - LAG)
        comm(t, always)
        x_copy(t).wait()

        @pl.when(t + 2 < images)
        def _():
            x_copy(t + 2).start()

        z_free(t - LAG)
        stage0(t)
        pair_copy(t).start()
        stage6(t - LAG)
        z_copy(t - LAG).start()

    @pl.loop(images, images + LAG)
    def _(t):
        stage6_ready(t - LAG)
        comm(t, guarded)
        z_free(t - LAG)
        stage6(t - LAG)
        z_copy(t - LAG).start()

    z_copy(images - 2).wait()
    z_copy(images - 1).wait()


def solution(mesh):
    n = mesh.shape["sp"]
    row_spec = P("dp", "sp", None)

    def local_layer(x, w1, b1, w2, b2, wc1, bc1, wc2, bc2, g1, o1, g2, o2):
        images, rows, chans = x.shape
        hid = w1.shape[1]
        own = b1.shape[0]
        wide = wc1.shape[1]
        chips = n // 2
        w1t = w1.T.reshape(chips, 2, own, rows).transpose(1, 0, 2, 3).reshape(hid, rows)
        vmem = pl.BlockSpec(memory_space=pltpu.VMEM)
        hbm = pl.BlockSpec(memory_space=pl.ANY)
        dma = pltpu.SemaphoreType.DMA
        return pl.pallas_call(
            functools.partial(layer_kernel, n),
            name="mixer_layer",
            out_shape=jax.ShapeDtypeStruct(x.shape, BF16),
            in_specs=[hbm] * 5 + [vmem] * 8,
            out_specs=hbm,
            scratch_shapes=[
                pltpu.VMEM((hid, rows), BF16),
                pltpu.VMEM((rows, hid), BF16),
                pltpu.VMEM((chans, wide), BF16),
                pltpu.VMEM((wide, chans), BF16),
                pltpu.VMEM((XS, rows, chans), BF16),
                pltpu.VMEM((rows, chans), BF16),
                pltpu.VMEM((hid // 2, chans), F32),
                pltpu.VMEM((3, hid // 2, chans), F32),
                pltpu.VMEM((2, hid // 2, chans), F32),
                pltpu.VMEM((2, own, chans // 2), BF16),
                pltpu.VMEM((2, 2, own, chans // 2), BF16),
                pltpu.VMEM((2, own, chans), BF16),
                pltpu.VMEM((2, 2, own, chans), BF16),
                pltpu.VMEM((GS, hid, chans), BF16),
                pltpu.VMEM((rows, chans), BF16),
                pltpu.VMEM((rows, chans), BF16),
                pltpu.VMEM((rows, CW), BF16),
                pltpu.VMEM((rows, CW), BF16),
                pltpu.VMEM((rows, chans), F32),
                pltpu.VMEM((2, rows, chans), BF16),
                dma((4,)), dma((XS,)), dma((2,)),
                dma, dma((2,)),
                dma((2,)), dma((2, 2)),
                dma((2,)), dma((2, 2)),
                dma((3,)), dma((2, 3)),
                dma((4,)), dma((2, 4)),
                dma, dma((2,)),
            ],
            compiler_params=pltpu.CompilerParams(collective_id=0, has_side_effects=True, vmem_limit_bytes=66_000_000),
        )(x, w1t, w2.T, wc1, wc2, b1[:, None], b2[:, None], bc1[None, :], bc2[None, :], g1[None, :], o1[None, :], g2[None, :], o2[None, :])

    in_specs = (row_spec, P("sp", None), P("sp"), P(None, "sp"), P("sp"), P(None, None), P(None), P(None, None), P(None),
                P(None), P(None), P(None), P(None))
    return jax.shard_map(local_layer, mesh=mesh, in_specs=in_specs, out_specs=row_spec, check_vma=False)
```

time: 589 us -> 274 us (0.47)
  waiting for transfers between devices: 254 us -> 0 us
  Pallas kernels: 0 us -> 249 us
  matrix products: 214 us -> 0 us
  local copies, waits for them, and re-layouts: 82.6 us -> 20.9 us
  other arithmetic: 23.8 us -> 0 us
  between operations: 13.6 us -> 0.02 us
    pallas_call x0 -> x1, Pallas kernels: none -> 249 us  [local_layer(): pl.pallas_call(functools.partial(layer_kernel, n), name='mixer_layer', ou...]
    dot_general x4 -> x0, matrix products: 214 us -> none  [the longest x1 86 us: channel_mix(): jnp.einsum('bsf,fc->bsc', ch_act, w_ch2, preferred_element_type=jnp.float32)]
    reduce_scatter x1 -> x0, waiting for transfers between devices: 171 us -> none  [local_layer(): lax.psum_scatter(part_pre, 'sp', scatter_dimension=1, tiled=True)]
    all_gather x1 -> x0, waiting for transfers between devices: 82.7 us -> none  [local_layer(): act_full = lax.all_gather(tok_act, 'sp', axis=1, tiled=True)]
    transpose x1, local copies, waits for them, and re-layouts: 33.1 us -> 0.85 us  [local_layer(): w1.T.reshape(chips, 2, own, rows).transpose(1, 0, 2, 3).reshape(hid, rows)]
    convert_element_type x1 -> x0, local copies, waits for them, and re-layouts: 21.5 us -> none  [channel_mix(): return (mid_wide + ch_out).astype(jnp.bfloat16)]
    reduce_sum x3 -> x0, other arithmetic: 18.7 us -> none  [the longest x2 12 us: layer_norm(): var_val = jnp.mean(centred * centred, axis=-1, keepdims=True)]
    unnamed x25 -> x3, local copies, waits for them, and re-layouts: 27.9 us -> 17.2 us
  transfers between devices with their start and end apart: 2 -> 0, of which waited for: 2 -> 0; matrix products, arithmetic and copies ran while one was open for 0% -> 0% of each run, Pallas kernels for 0% -> 0%
where the time goes in v1:
time: 274 us; the launch traced here: 270 us
  Pallas kernels  249 us (91%)
  local copies, waits for them, and re-layouts  20.9 us (8%)
    pallas_call x1, Pallas kernels, local_layer(): pl.pallas_call(functools.partial(layer_kernel, n), name='mixer_layer', ou...  249 us
    unnamed x3, local copies, waits for them, and re-layouts  17.2 us

profile of v1, /device:TPU:81, one launch (start us, length us, event | category | flops | bytes accessed | tf_op | source)
XLA Modules:
  0.0 270.1 jit_solution(17244416913165320083)
XLA Ops:
  0.0 1.3 copy.20.b1_ref
  1.3 1.5 copy.21.b2_ref
  2.9 1.3 copy.17
  4.1 0.8 copy.18
  5.0 2.0 copy.19
  7.0 249.1 %mixer_layer.1 = bf16[16,512,1024]{2,1,0:T(8,128)(2,1)} custom-call(bf16[16,512,1024]{2,1,0:T(8,128)(2,1)} %x_hbm.1, bf16[512,512]{1,0:T(8,128)(2,1)} %bitcast.15, bf16[512,512]{1,0:T(8,128)(2,1)} %bitcast.16, bf16[1024,4096]{1,0:T(8,128)(2,1)} %wc1_hbm.1, bf16[4096,1024]{1,0:T(8,128)(2,1)} %wc2_hbm.1, f32[64,1]{1,0:T(8,128)} %copy.20.b1_ref, ...), custom_call_target="tpu_custom_call" | custom-call | tf_op jit(solution)/shard_map/mixer_layer/pallas_call | solution.py:310
  256.2 13.9 %copy.23 = bf16[16,512,1024]{2,1,0:T(8,128)(2,1)} copy(bf16[16,512,1024]{2,1,0:T(8,128)(2,1)} %mixer_layer.1) | data formatting | bytes 33554432
